TPU v7x, 32 devices: a whole 2x2x4 slice. The times are simulated.
32 devices in a mesh: dom: 8 (over y, x, core), feat: 4 (over z).
Axes of the slice: x: 2, y: 2, z: 4, core: 2. Of those that a mesh axis runs over, the one named last changes fastest.
Arguments:
- features: bfloat16 [128, 131072], P('feat', 'dom'), may hold values from -6 to 6
- seed_rows: int32 [2048], P('dom'), may hold values from 0 to 16383
- want_rows: int32 [8, 8, 128], P('dom'), may hold values from 0 to 16383
- live_counts: int32 [8, 8], P('dom'), may hold values from 1 to 128, as said below
- hop_one: int32 [15, 2048], P(None, 'dom'), may hold values from 0 to 1023, as said below
- hop_two: int32 [10, 15, 2048], P(None, None, 'dom'), may hold values from 0 to 1023, as said below
- w1_self: bfloat16 [256, 128], replicated, may hold values from -0.5 to 0.5
- w1_neigh: bfloat16 [256, 128], replicated, may hold values from -0.5 to 0.5
- b1: float32 [256], P('feat'), may hold values from -4 to 4
- w2_self: bfloat16 [256, 256], P(None, 'feat'), may hold values from -0.375 to 0.375
- w2_neigh: bfloat16 [256, 256], P(None, 'feat'), may hold values from -0.375 to 0.375
- b2: float32 [256], P('feat'), may hold values from -4 to 4
Outputs:
- embed: float32 [256, 2048], P('feat', 'dom')
Inputs may be any that keep to these rules, and one draw needn't show every extreme that they name: `want_rows`: slots at or beyond live_counts[r, o] are ignored. `live_counts`: in every draw a quarter of the owners, every fourth one from a drawn offset, receive all 128 slots from every requester. `hop_one`: each entry is o * 128 + c, a position in the buffer of the requester that holds seed s, with c < live_counts of that requester and owner o. `hop_two`: each entry is o * 128 + c, a position in the buffer of the requester that holds seed s, with c < live_counts of that requester and owner o.
All inputs are finite; a program needn't handle non-finite values.
Results may differ from a plain program's by a relative error of at most 0.00036.
Values may be sent and summed in bfloat16 or wider, within the bound.
A program may use at most 64 MiB of HBM per device.

v0:
```python
import jax
import jax.numpy as jnp
from jax import lax
from jax.sharding import PartitionSpec as P

OUT = 256
FAN1 = 15
FAN2 = 10
CAP = 128


def aggregate_counts(fetched, hop_one, hop_two):
    feat_dev, slots = fetched.shape
    width = CAP * 4
    first = hop_one.reshape(1, -1)
    second = hop_two.reshape(FAN2, -1)
    columns = first.shape[1]

    def add_block(blocks, carry):
        start = blocks * width
        piece = lax.dynamic_slice_in_dim(fetched, start, width, 1)
        place = start + lax.broadcasted_iota(jnp.int32, (width, 1), 0)
        pick_one = (first == place).astype(jnp.bfloat16)
        pick_two = jnp.zeros((width, columns), jnp.bfloat16)
        for sample in range(FAN2):
            pick_two = pick_two + (second[sample : sample + 1] == place).astype(jnp.bfloat16)
        own_sum = carry[0] + jnp.dot(piece, pick_one, preferred_element_type=jnp.float32)
        mean_sum = carry[1] + jnp.dot(piece, pick_two, preferred_element_type=jnp.float32)
        return (own_sum, mean_sum)

    zeros = jnp.zeros((feat_dev, columns), jnp.float32)
    own_sum, mean_sum = lax.fori_loop(0, slots // width, add_block, (zeros, zeros))
    return (own_sum.astype(jnp.bfloat16), (mean_sum * (1.0 / FAN2)).astype(jnp.bfloat16))


def per_device(
    features,
    seed_rows,
    want_rows,
    live_counts,
    hop_one,
    hop_two,
    w1_self,
    w1_neigh,
    b1,
    w2_self,
    w2_neigh,
    b2,
):
    feat_dev = features.shape[0]
    seed_dev = seed_rows.shape[0]
    hid_dev = b1.shape[0]
    served = jnp.take(
        features,
        lax.all_to_all(want_rows, "dom", split_axis=1, concat_axis=0, tiled=True)[:, 0, :],
        axis=1,
    )
    returned = lax.all_to_all(served, "dom", split_axis=1, concat_axis=1, tiled=True)
    slot_ids = lax.broadcasted_iota(jnp.int32, (1, returned.shape[2]), 1)
    live_slots = slot_ids < live_counts[0][:, None]
    fetched = jnp.where(live_slots[None], returned, jnp.zeros((), jnp.bfloat16)).reshape(
        feat_dev, -1
    )
    x_one, m_two = aggregate_counts(fetched, hop_one, hop_two)
    x_seed = jnp.take(features, seed_rows, axis=1)
    m_one = jnp.sum(x_one.reshape(feat_dev, FAN1, seed_dev), axis=1, dtype=jnp.float32)
    m_one = (m_one * (1.0 / FAN1)).astype(jnp.bfloat16)
    selves = jnp.concatenate([x_one, x_seed], axis=1)
    means = jnp.concatenate([m_two, m_one], axis=1)
    hid_start = lax.axis_index("feat") * hid_dev
    self_rows = lax.dynamic_slice_in_dim(w1_self, hid_start, hid_dev, 0)
    neigh_rows = lax.dynamic_slice_in_dim(w1_neigh, hid_start, hid_dev, 0)
    self_part = self_rows
    neigh_part = neigh_rows
    total = jnp.dot(
        self_part,
        lax.all_gather(selves, "feat", axis=0, tiled=True),
        preferred_element_type=jnp.float32,
    )
    pre = total + jnp.dot(
        neigh_part,
        lax.all_gather(means, "feat", axis=0, tiled=True),
        preferred_element_type=jnp.float32,
    )
    hidden = jnp.maximum(pre + b1[:, None], 0.0)
    hop_cols = FAN1 * seed_dev
    h_one = hidden[:, :hop_cols]
    h_seed = hidden[:, hop_cols:]
    g_mean = jnp.sum(h_one.reshape(hid_dev, FAN1, seed_dev), axis=1) * (1.0 / FAN1)
    second_self = w2_self.astype(jnp.float32)
    second_neigh = w2_neigh.astype(jnp.float32)
    self_part = second_self
    neigh_part = second_neigh
    total = jnp.dot(
        self_part, h_seed, precision=lax.Precision.HIGHEST, preferred_element_type=jnp.float32
    )
    z_out = (
        lax.psum_scatter(
            total
            + jnp.dot(
                neigh_part,
                g_mean,
                precision=lax.Precision.HIGHEST,
                preferred_element_type=jnp.float32,
            ),
            "feat",
            scatter_dimension=0,
            tiled=True,
        )
        + b2[:, None]
    )
    square = lax.psum(jnp.sum(z_out * z_out, axis=0), "feat")
    return z_out * lax.rsqrt(square * (1.0 / OUT) + 1.0)


def solution(mesh):
    return jax.shard_map(
        per_device,
        mesh=mesh,
        in_specs=(
            P("feat", "dom"),
            P("dom"),
            P("dom", None, None),
            P("dom", None),
            P(None, "dom"),
            P(None, None, "dom"),
            P(),
            P(),
            P("feat"),
            P(None, "feat"),
            P(None, "feat"),
            P("feat"),
        ),
        out_specs=P("feat", "dom"),
        check_vma=False,
    )
```

profile of v0, /device:TPU:0, one launch (start us, length us, event | category | flops | bytes accessed | tf_op | source)
XLA Modules:
  0.0 154.3 jit_solution(16646595926999399263)
XLA Ops:
  6.5 5.3 %all-to-all-start = ((s32[1,8,128]{2,0,1:T(1,128)}), s32[1,8,128]{2,0,1:T(1,128)S(1)}, u32[]{:S(2)}, u32[]{:S(2)}) async-start(s32[1,8,128]{2,0,1:T(1,128)} %bitcast.38), calls=%async_computation | async-start | bytes 8192 | tf_op jit(solution)/shard_map/all_to_all | solution.py:55
  11.9 0.7 compare_select_fusion.2
  12.6 0.7 compare_and_fusion.1
  13.2 4.6 %copy.30 = bf16[32,16384]{0,1:T(8,128)(2,1)} copy(bf16[32,16384]{1,0:T(8,128)(2,1)} %param.14) | data formatting | bytes 2097152 | tf_op args[0]
  17.8 3.5 %gather_fusion.1 = bf16[256,32]{1,0:T(8,128)(2,1)S(1)} fusion(bf16[32,16384]{0,1:T(8,128)(2,1)} %copy.30, s32[1024]{0:T(1024)S(1)} %pad_clamp_fusion), kind=kCustom, calls=%fused_computation.1 | custom fusion | bytes 33792 | tf_op jit(solution)/shard_map/jit(_take)/gather | solution.py:65
  21.4 5.6 %gather_fusion = bf16[1024,32]{1,0:T(8,128)(2,1)S(1)} fusion(bf16[32,16384]{0,1:T(8,128)(2,1)} %copy.30, s32[1024]{0:T(1024)S(1)} %fusion.43), kind=kCustom, calls=%fused_computation | custom fusion | bytes 135168 | tf_op jit(solution)/shard_map/jit(_take)/gather | solution.py:53
  27.2 0.6 select_bitcast_fusion.1
  27.8 4.2 %all-to-all-start.1 = ((bf16[32,8,128]{2,0,1:T(8,128)(2,1)}), bf16[32,8,128]{2,0,1:T(8,128)(2,1)S(1)}, u32[]{:S(2)}, u32[]{:S(2)}) async-start(bf16[32,8,128]{2,0,1:T(8,128)(2,1)} %select_bitcast_fusion.1), calls=%async_computation.1 | async-start | bytes 131072 | tf_op jit(solution)/shard_map/all_to_all | solution.py:58
  32.0 0.2 all-gather.3.cloned.1.call-start
  32.6 4.4 %all-to-all-done.1 = bf16[32,8,128]{2,0,1:T(8,128)(2,1)S(1)} async-done(((bf16[32,8,128]{2,0,1:T(8,128)(2,1)}), bf16[32,8,128]{2,0,1:T(8,128)(2,1)S(1)}, u32[]{:S(2)}, u32[]{:S(2)}) %all-to-all-start.1) | async-done | bytes 65568 | tf_op jit(solution)/shard_map/all_to_all | solution.py:58
  37.1 19.3 %while.16 = (s32[]{:T(128)}, f32[32,3840]{1,0:T(8,128)S(1)}, f32[32,3840]{1,0:T(8,128)S(1)}, bf16[32,1024]{1,0:T(8,128)(2,1)S(1)}, s32[1,3840]{1,0:T(1,128)S(1)}...) while((s32[]{:T(128)}, f32[32,3840]{1,0:T(8,128)S(1)}, ...), condition=%wide.region_1.2_spmd.clone, body=%wide.region_0.1_spmd.clone.sunk | while | flops 311132672 | bytes 2556086 | solution.py:32
  37.1 1.5 fusion.60
  38.6 0.4 slice_reduce_fusion.11
  39.0 7.7 %convolution_add_fusion.4 = f32[32,3840]{1,0:T(8,128)S(1)} fusion(s32[3840]{0:T(1024)S(1)} %get-tuple-element.207, s32[3840]{0:T(1024)S(1)} %get-tuple-element.208, s32[3840]{0:T(1024)S(1)} %get-tuple-element.209, s32[3840]{0:T(1024)S(1)} %get-tuple-element.210, s32[3840]{0:T(1024)S(1)} %get-tuple-element.211, s32[3840]{0:T(1024)S(1)} %get-tuple-element.212, ...), kind=kOutput, calls=%fused_computation.14.clone.1 | convolution fusion | flops 183091200 | bytes 1181701 | tf_op jit(solution)/shard_map/while/body/eval_jaxpr/dot_general | solution.py:28
  46.8 1.5 fusion.60
  48.3 0.4 slice_reduce_fusion.11
  48.7 7.7 %convolution_add_fusion.4 = f32[32,3840]{1,0:T(8,128)S(1)} fusion(s32[3840]{0:T(1024)S(1)} %get-tuple-element.207, s32[3840]{0:T(1024)S(1)} %get-tuple-element.208, s32[3840]{0:T(1024)S(1)} %get-tuple-element.209, s32[3840]{0:T(1024)S(1)} %get-tuple-element.210, s32[3840]{0:T(1024)S(1)} %get-tuple-element.211, s32[3840]{0:T(1024)S(1)} %get-tuple-element.212, ...), kind=kOutput, calls=%fused_computation.14.clone.1 | convolution fusion | flops 183091200 | bytes 1181701 | tf_op jit(solution)/shard_map/while/body/eval_jaxpr/dot_general | solution.py:28
  56.5 0.2 reshape.90
  56.7 0.7 pad_maximum_fusion
  57.7 0.7 pad_maximum_fusion.1
  58.5 26.5 %all-gather.3.cloned.1.call-done = bf16[128,4096]{1,0:T(8,128)(2,1)} async-done(((bf16[32,4096]{1,0:T(8,128)(2,1)}), bf16[128,4096]{1,0:T(8,128)(2,1)}) %all-gather.3.cloned.1.call-update) | async-done | bytes 1048592 | tf_op jit(solution)/shard_map/all_gather | solution.py:77
  84.9 1.5 fusion.40
  86.5 27.4 %all-gather.5.cloned.1.call-done = bf16[128,4096]{1,0:T(8,128)(2,1)} async-done(((bf16[32,4096]{1,0:T(8,128)(2,1)}), bf16[128,4096]{1,0:T(8,128)(2,1)}) %all-gather.5.cloned.1.call-update) | async-done | bytes 1048592 | tf_op jit(solution)/shard_map/all_gather | solution.py:82
  113.9 1.5 fusion.33
  115.5 0.3 fusion.35
  115.9 0.3 reshape.89
  116.4 0.3 fusion.34
  116.7 0.8 copy.36
  117.5 19.5 %reduce-scatter.4.cloned.1.call-done = f32[64,256]{1,0:T(8,128)} async-done(((f32[256,256]{1,0:T(8,128)}), f32[64,256]{1,0:T(8,128)}) %reduce-scatter.4.cloned.1.call-update) | async-done | bytes 65552
  137.1 0.9 copy.37
  138.1 8.8 %psum.7 = f32[256]{0:T(256)S(1)} all-reduce(f32[256]{0:T(256)S(1)} %multiply_reduce_fusion), channel_id=1, replica_groups=mesh['dom'=8,'feat'=4] {'feat'}, use_global_device_ids=true, to_apply=%region_6.7 | all-reduce | flops 256 | bytes 2048 | tf_op jit(solution)/shard_map/psum | solution.py:112
  147.1 0.7 copy.35
  (48 shorter events, 1.5 us)
Async XLA Ops:
  6.5 78.4 %copy-start = (bf16[256,128]{1,0:T(8,128)(2,1)S(1)}, bf16[256,128]{1,0:T(8,128)(2,1)}, u32[]{:S(2)}) copy-start(bf16[256,128]{1,0:T(8,128)(2,1)} %param.20) | copy-start | bytes 196612
  6.5 25.7 %copy-start.7 = (s32[1,8]{1,0:T(1,128)S(1)}, s32[1,8]{1,0:T(1,128)}, u32[]{:S(2)}) copy-start(s32[1,8]{1,0:T(1,128)} %param.17) | copy-start | bytes 100
  6.5 25.9 %copy-start.4 = (s32[15,256]{1,0:T(8,128)S(1)}, s32[15,256]{1,0:T(8,128)}, u32[]{:S(2)}) copy-start(s32[15,256]{1,0:T(8,128)} %param.18) | copy-start | bytes 46084
  6.5 25.9 %copy-start.1 = (s32[10,15,256]{2,1,0:T(8,128)S(1)}, s32[10,15,256]{2,1,0:T(8,128)}, u32[]{:S(2)}) copy-start(s32[10,15,256]{2,1,0:T(8,128)} %param.19) | copy-start | bytes 460804
  6.5 14.9 %all-to-all-start = ((s32[1,8,128]{2,0,1:T(1,128)}), s32[1,8,128]{2,0,1:T(1,128)S(1)}, u32[]{:S(2)}, u32[]{:S(2)}) async-start(s32[1,8,128]{2,0,1:T(1,128)} %bitcast.38), calls=%async_computation | async-start | bytes 8192 | tf_op jit(solution)/shard_map/all_to_all | solution.py:55
  27.8 9.2 %all-to-all-start.1 = ((bf16[32,8,128]{2,0,1:T(8,128)(2,1)}), bf16[32,8,128]{2,0,1:T(8,128)(2,1)S(1)}, u32[]{:S(2)}, u32[]{:S(2)}) async-start(bf16[32,8,128]{2,0,1:T(8,128)(2,1)} %select_bitcast_fusion.1), calls=%async_computation.1 | async-start | bytes 131072 | tf_op jit(solution)/shard_map/all_to_all | solution.py:58
  32.0 52.9 %all-gather.3.cloned.1.call-start = ((), (), s32[]{:S(2)}) async-start(), calls=%async_computation.3 | async-start | bytes 1310720 | tf_op jit(solution)/shard_map/all_gather | solution.py:77
  56.4 57.5 %copy-start.6 = (f32[64]{0:T(128)S(1)}, f32[64]{0:T(128)}, u32[]{:S(2)}) copy-start(f32[64]{0:T(128)} %param.22) | copy-start | bytes 772
  57.4 56.5 %all-gather.5.cloned.1.call-start = ((), (), s32[]{:S(2)}) async-start(), calls=%async_computation.4 | async-start | bytes 1310720 | tf_op jit(solution)/shard_map/all_gather | solution.py:82
  57.6 57.9 %copy-start.3 = (bf16[256,64]{0,1:T(8,128)(2,1)S(1)}, bf16[256,64]{0,1:T(8,128)(2,1)}, u32[]{:S(2)}) copy-start(bf16[256,64]{0,1:T(8,128)(2,1)} %param.23) | copy-start | bytes 98308
  58.4 78.7 %reduce-scatter.4.cloned.1.call-start = ((), (), s32[]{:S(2)}) async-start(), calls=%async_computation.5 | async-start | bytes 327680
  86.4 29.9 %copy-start.2 = (bf16[256,64]{0,1:T(8,128)(2,1)S(1)}, bf16[256,64]{0,1:T(8,128)(2,1)}, u32[]{:S(2)}) copy-start(bf16[256,64]{0,1:T(8,128)(2,1)} %param.24) | copy-start | bytes 98308
  115.4 22.6 %copy-start.5 = (f32[64]{0:T(128)S(1)}, f32[64]{0:T(128)}, u32[]{:S(2)}) copy-start(f32[64]{0:T(128)} %param.25) | copy-start | bytes 772
Sparse Core Ops, SparseCore 0:
  57.5 27.3 all-gather.2
  86.5 27.3 all-gather.4
  117.7 19.3 reduce-scatter.3
where the time goes:
time: 155 us; the launch traced here: 154 us
  waiting for transfers between devices  77.9 us (50%)
  matrix products  22 us (14%)
  local copies, waits for them, and re-layouts  17.9 us (12%)
  between operations  13.4 us (9%)
  starting transfers between devices  9.84 us (6%)
  blocking collectives  8.85 us (6%)
  other arithmetic  4.35 us (3%)
    all_gather x1, waiting for transfers between devices, per_device(): lax.all_gather(means, 'feat', axis=0, tiled=True)  27.4 us
    all_gather x1, waiting for transfers between devices, per_device(): lax.all_gather(selves, 'feat', axis=0, tiled=True)  26.5 us
    unnamed x4, waiting for transfers between devices  19.6 us
    dot_general x2, matrix products, add_block(): jnp.dot(piece, pick_two, preferred_element_type=jnp.float32)  15.4 us
    psum x1, blocking collectives, per_device(): square = lax.psum(jnp.sum(z_out * z_out, axis=0), 'feat')  8.85 us
    unnamed x22, local copies, waits for them, and re-layouts  6.56 us
    gather x2, local copies, waits for them, and re-layouts, per_device(): jnp.take(features, lax.all_to_all(want_rows, 'dom', split_axis=1, concat_...  5.73 us
    all_to_all x1, starting transfers between devices, per_device(): lax.all_to_all(want_rows, 'dom', split_axis=1, concat_axis=0, tiled=True)  5.34 us
  transfers between devices with their start and end apart: 5, of which 4 were waited for; matrix products, arithmetic and copies ran while one was open for 8% of the time, Pallas kernels for 0%

commit v1 on v0

--- a/solution.py
+++ b/solution.py
@@ -7,6 +7,18 @@
 FAN1 = 15
 FAN2 = 10
 CAP = 128
+
+
+def ring_gather(array, axis, dim):
+    ways, here, step = (lax.axis_size(axis), lax.axis_index(axis), array.shape[dim])
+    lengths = [n * ways if d == dim else n for d, n in enumerate(array.shape)]
+    full = lax.dynamic_update_slice_in_dim(
+        jnp.zeros(lengths, array.dtype), array, here * step, axis=dim
+    )
+    for far in range(1, ways):
+        array = lax.ppermute(array, axis, [(d, (d + 1) % ways) for d in range(ways)])
+        full = lax.dynamic_update_slice_in_dim(full, array, (here - far) % ways * step, axis=dim)
+    return full
 
 
 def aggregate_counts(fetched, hop_one, hop_two):
@@ -78,9 +90,7 @@
         preferred_element_type=jnp.float32,
     )
     pre = total + jnp.dot(
-        neigh_part,
-        lax.all_gather(means, "feat", axis=0, tiled=True),
-        preferred_element_type=jnp.float32,
+        neigh_part, ring_gather(means, "feat", 0), preferred_element_type=jnp.float32
     )
     hidden = jnp.maximum(pre + b1[:, None], 0.0)
     hop_cols = FAN1 * seed_dev

time: 155 us -> 138 us (0.89)
  waiting for transfers between devices: 77.9 us -> 59.2 us
  starting transfers between devices: 9.84 us -> 12.6 us
    ppermute x0 -> x3, waiting for transfers between devices: none -> 37.3 us  [ring_gather(): lax.ppermute(array, axis, [(d, (d + 1) % ways) for d in range(ways)])]
    all_gather x1 -> x0, waiting for transfers between devices: 27.4 us -> none  [per_device(): lax.all_gather(means, 'feat', axis=0, tiled=True)]
    all_gather x1, waiting for transfers between devices: 26.5 us -> 0.02 us  [per_device(): lax.all_gather(selves, 'feat', axis=0, tiled=True)]
    ppermute x0 -> x3, starting transfers between devices: none -> 2.81 us  [ring_gather(): lax.ppermute(array, axis, [(d, (d + 1) % ways) for d in range(ways)])]
    unnamed x4 -> x3, waiting for transfers between devices: 19.6 us -> 17.5 us
  transfers between devices with their start and end apart: 5 -> 7, of which waited for: 4 -> 5; matrix products, arithmetic and copies ran while one was open for 8% -> 8% of each run, Pallas kernels for 0% -> 0%
where the time goes in v1:
time: 138 us
  waiting for transfers between devices  59.2 us (43%)
  matrix products  21.5 us (16%)
  local copies, waits for them, and re-layouts  18 us (13%)
  between operations  13.8 us (10%)
  starting transfers between devices  12.6 us (9%)
  blocking collectives  8.74 us (6%)
  other arithmetic  3.66 us (3%)
    ppermute x3, waiting for transfers between devices, ring_gather(): lax.ppermute(array, axis, [(d, (d + 1) % ways) for d in range(ways)])  37.3 us
    unnamed x3, waiting for transfers between devices  17.5 us
    dot_general x2, matrix products, add_block(): jnp.dot(piece, pick_two, preferred_element_type=jnp.float32)  15.4 us
    psum x1, blocking collectives, per_device(): square = lax.psum(jnp.sum(z_out * z_out, axis=0), 'feat')  8.74 us
    unnamed x22, local copies, waits for them, and re-layouts  6.56 us
    gather x2, local copies, waits for them, and re-layouts, per_device(): jnp.take(features, lax.all_to_all(want_rows, 'dom', split_axis=1, concat_...  5.73 us
    all_to_all x1, starting transfers between devices, per_device(): lax.all_to_all(want_rows, 'dom', split_axis=1, concat_axis=0, tiled=True)  5.34 us
    all_to_all x1, waiting for transfers between devices, per_device(): lax.all_to_all(served, 'dom', split_axis=1, concat_axis=1, tiled=True)  4.4 us
  transfers between devices with their start and end apart: 7, of which 5 were waited for; matrix products, arithmetic and copies ran while one was open for 8% of the time, Pallas kernels for 0%

profile of v1, /device:TPU:0, one launch (start us, length us, event | category | flops | bytes accessed | tf_op | source)
XLA Modules:
  0.0 137.6 jit_solution(2198998284059500569)
XLA Ops:
  6.5 5.3 %all-to-all-start = ((s32[1,8,128]{2,0,1:T(1,128)}), s32[1,8,128]{2,0,1:T(1,128)S(1)}, u32[]{:S(2)}, u32[]{:S(2)}) async-start(s32[1,8,128]{2,0,1:T(1,128)} %bitcast.38), calls=%async_computation | async-start | bytes 8192 | tf_op jit(solution)/shard_map/all_to_all | solution.py:67
  11.9 0.7 compare_select_fusion.2
  12.6 0.7 compare_and_fusion.1
  13.2 4.6 %copy.30 = bf16[32,16384]{0,1:T(8,128)(2,1)} copy(bf16[32,16384]{1,0:T(8,128)(2,1)} %param.14) | data formatting | bytes 2097152 | tf_op args[0]
  17.8 3.5 %gather_fusion.1 = bf16[256,32]{1,0:T(8,128)(2,1)S(1)} fusion(bf16[32,16384]{0,1:T(8,128)(2,1)} %copy.30, s32[1024]{0:T(1024)S(1)} %pad_clamp_fusion), kind=kCustom, calls=%fused_computation.1 | custom fusion | bytes 33792 | tf_op jit(solution)/shard_map/jit(_take)/gather | solution.py:77
  21.4 5.6 %gather_fusion = bf16[1024,32]{1,0:T(8,128)(2,1)S(1)} fusion(bf16[32,16384]{0,1:T(8,128)(2,1)} %copy.30, s32[1024]{0:T(1024)S(1)} %fusion.43), kind=kCustom, calls=%fused_computation | custom fusion | bytes 135168 | tf_op jit(solution)/shard_map/jit(_take)/gather | solution.py:65
  27.2 0.6 select_bitcast_fusion.1
  27.8 4.2 %all-to-all-start.1 = ((bf16[32,8,128]{2,0,1:T(8,128)(2,1)}), bf16[32,8,128]{2,0,1:T(8,128)(2,1)S(1)}, u32[]{:S(2)}, u32[]{:S(2)}) async-start(bf16[32,8,128]{2,0,1:T(8,128)(2,1)} %select_bitcast_fusion.1), calls=%async_computation.1 | async-start | bytes 131072 | tf_op jit(solution)/shard_map/all_to_all | solution.py:70
  32.6 4.4 %all-to-all-done.1 = bf16[32,8,128]{2,0,1:T(8,128)(2,1)S(1)} async-done(((bf16[32,8,128]{2,0,1:T(8,128)(2,1)}), bf16[32,8,128]{2,0,1:T(8,128)(2,1)S(1)}, u32[]{:S(2)}, u32[]{:S(2)}) %all-to-all-start.1) | async-done | bytes 65568 | tf_op jit(solution)/shard_map/all_to_all | solution.py:70
  37.1 19.3 %while.16 = (s32[]{:T(128)}, f32[32,3840]{1,0:T(8,128)S(1)}, f32[32,3840]{1,0:T(8,128)S(1)}, bf16[32,1024]{1,0:T(8,128)(2,1)S(1)}, s32[1,3840]{1,0:T(1,128)S(1)}...) while((s32[]{:T(128)}, f32[32,3840]{1,0:T(8,128)S(1)}, ...), condition=%wide.region_1.2_spmd.clone, body=%wide.region_0.1_spmd.clone.sunk | while | flops 311132672 | bytes 2556086 | solution.py:44
  37.1 1.5 %fusion.60 = f32[32,3840]{1,0:T(8,128)S(1)} fusion(s32[3840]{0:T(1024)S(1)} %reduce.24, s32[512]{0:T(512)S(1)} %iota_add_fusion.2, f32[32,3840]{1,0:T(8,128)S(1)} %get-tuple-element.230, pred[]{:T(512)S(6)} %compare.6, bf16[32,1024]{1,0:T(8,128)(2,1)S(1)} %get-tuple-element.242, s32[]{:T(128)S(6)} %select_n.104), kind=kOutput, calls=%fused_computation.15.clone.1 | convolution fusion | flops 128040960 | bytes 1034245 | tf_op jit(solution)/shard_map/while/body/eval_jaxpr/dot_general | solution.py:39
  38.6 0.4 slice_reduce_fusion.11
  39.0 7.7 %convolution_add_fusion.4 = f32[32,3840]{1,0:T(8,128)S(1)} fusion(s32[3840]{0:T(1024)S(1)} %get-tuple-element.209, s32[3840]{0:T(1024)S(1)} %get-tuple-element.210, s32[3840]{0:T(1024)S(1)} %get-tuple-element.211, s32[3840]{0:T(1024)S(1)} %get-tuple-element.212, s32[3840]{0:T(1024)S(1)} %get-tuple-element.213, s32[3840]{0:T(1024)S(1)} %get-tuple-element.214, ...), kind=kOutput, calls=%fused_computation.14.clone.1 | convolution fusion | flops 183091200 | bytes 1181701 | tf_op jit(solution)/shard_map/while/body/eval_jaxpr/dot_general | solution.py:40
  46.8 1.5 %fusion.60 = f32[32,3840]{1,0:T(8,128)S(1)} fusion(s32[3840]{0:T(1024)S(1)} %reduce.24, s32[512]{0:T(512)S(1)} %iota_add_fusion.2, f32[32,3840]{1,0:T(8,128)S(1)} %get-tuple-element.230, pred[]{:T(512)S(6)} %compare.6, bf16[32,1024]{1,0:T(8,128)(2,1)S(1)} %get-tuple-element.242, s32[]{:T(128)S(6)} %select_n.104), kind=kOutput, calls=%fused_computation.15.clone.1 | convolution fusion | flops 128040960 | bytes 1034245 | tf_op jit(solution)/shard_map/while/body/eval_jaxpr/dot_general | solution.py:39
  48.3 0.4 slice_reduce_fusion.11
  48.7 7.7 %convolution_add_fusion.4 = f32[32,3840]{1,0:T(8,128)S(1)} fusion(s32[3840]{0:T(1024)S(1)} %get-tuple-element.209, s32[3840]{0:T(1024)S(1)} %get-tuple-element.210, s32[3840]{0:T(1024)S(1)} %get-tuple-element.211, s32[3840]{0:T(1024)S(1)} %get-tuple-element.212, s32[3840]{0:T(1024)S(1)} %get-tuple-element.213, s32[3840]{0:T(1024)S(1)} %get-tuple-element.214, ...), kind=kOutput, calls=%fused_computation.14.clone.1 | convolution fusion | flops 183091200 | bytes 1181701 | tf_op jit(solution)/shard_map/while/body/eval_jaxpr/dot_general | solution.py:40
  57.0 1.6 %collective-permute-start = (bf16[32,4096]{1,0:T(8,128)(2,1)S(1)}, bf16[32,4096]{1,0:T(8,128)(2,1)S(1)}, u32[]{:S(2)}, u32[]{:S(2)}) collective-permute-start(bf16[32,4096]{1,0:T(8,128)(2,1)S(1)} %get-tuple-element.160), channel_id=1, source_target_pairs={{0,1},{1,2},{2,3},{3,0},{4,5},{5,6},{6,7},{7,4},{8,9},{9,10},{10,1... | collective-permute-start | bytes 786440 | tf_op jit(solution)/shard_map/ppermute | solution.py:19
  58.6 0.7 pad_maximum_fusion
  59.5 7.3 %collective-permute-done = bf16[32,4096]{1,0:T(8,128)(2,1)S(1)} collective-permute-done((bf16[32,4096]{1,0:T(8,128)(2,1)S(1)}, bf16[32,4096]{1,0:T(8,128)(2,1)S(1)}, u32[]{:S(2)}, u32[]{:S(2)}) %collective-permute-start) | collective-permute-done | bytes 262176 | tf_op jit(solution)/shard_map/ppermute | solution.py:19
  66.8 15.8 %collective-permute-done.1 = bf16[32,4096]{1,0:T(8,128)(2,1)S(1)} collective-permute-done((bf16[32,4096]{1,0:T(8,128)(2,1)S(1)}, bf16[32,4096]{1,0:T(8,128)(2,1)S(1)}, u32[]{:S(2)}, u32[]{:S(2)}) %collective-permute-start.1) | collective-permute-done | bytes 262176 | tf_op jit(solution)/shard_map/ppermute | solution.py:19
  82.6 1.2 collective-permute-start.2
  83.8 14.2 %collective-permute-done.2 = bf16[32,4096]{1,0:T(8,128)(2,1)S(1)} collective-permute-done((bf16[32,4096]{1,0:T(8,128)(2,1)S(1)}, bf16[32,4096]{1,0:T(8,128)(2,1)S(1)}, u32[]{:S(2)}, u32[]{:S(2)}) %collective-permute-start.2) | collective-permute-done | bytes 262176 | tf_op jit(solution)/shard_map/ppermute | solution.py:19
  98.1 1.5 %fusion.40 = f32[64,4096]{1,0:T(8,128)S(1)} fusion(bf16[128,4096]{1,0:T(8,128)(2,1)} %all-gather.2.cloned.1.call-done, bf16[256,128]{1,0:T(8,128)(2,1)S(1)} %copy-done, s32[]{:T(128)S(6)} %select_n.71), kind=kOutput, calls=%fused_computation.73 | convolution fusion | flops 67108864 | bytes 2113540 | tf_op jit(solution)/shard_map/dot_general | solution.py:87
  99.6 1.0 fusion.33
  100.7 0.3 fusion.35
  101.1 0.3 reshape.89
  101.6 0.3 fusion.34
  101.9 0.8 copy.36
  102.8 17.4 %reduce-scatter.4.cloned.1.call-done = f32[64,256]{1,0:T(8,128)} async-done(((f32[256,256]{1,0:T(8,128)}), f32[64,256]{1,0:T(8,128)}) %reduce-scatter.4.cloned.1.call-update) | async-done | bytes 65552
  120.2 0.9 copy.37
  121.2 8.7 %psum.7 = f32[256]{0:T(256)S(1)} all-reduce(f32[256]{0:T(256)S(1)} %multiply_reduce_fusion), channel_id=1, replica_groups=mesh['dom'=8,'feat'=4] {'feat'}, use_global_device_ids=true, to_apply=%region_6.7 | all-reduce | flops 256 | bytes 2048 | tf_op jit(solution)/shard_map/psum | solution.py:122
  130.1 0.7 copy.35
  (55 shorter events, 2.1 us)
Async XLA Ops:
  6.5 91.5 %copy-start = (bf16[256,128]{1,0:T(8,128)(2,1)S(1)}, bf16[256,128]{1,0:T(8,128)(2,1)}, u32[]{:S(2)}) copy-start(bf16[256,128]{1,0:T(8,128)(2,1)} %param.20) | copy-start | bytes 196612
  6.5 25.7 %copy-start.7 = (s32[1,8]{1,0:T(1,128)S(1)}, s32[1,8]{1,0:T(1,128)}, u32[]{:S(2)}) copy-start(s32[1,8]{1,0:T(1,128)} %param.17) | copy-start | bytes 100
  6.5 25.9 %copy-start.4 = (s32[15,256]{1,0:T(8,128)S(1)}, s32[15,256]{1,0:T(8,128)}, u32[]{:S(2)}) copy-start(s32[15,256]{1,0:T(8,128)} %param.18) | copy-start | bytes 46084
  6.5 25.9 %copy-start.1 = (s32[10,15,256]{2,1,0:T(8,128)S(1)}, s32[10,15,256]{2,1,0:T(8,128)}, u32[]{:S(2)}) copy-start(s32[10,15,256]{2,1,0:T(8,128)} %param.19) | copy-start | bytes 460804
  6.5 14.9 %all-to-all-start = ((s32[1,8,128]{2,0,1:T(1,128)}), s32[1,8,128]{2,0,1:T(1,128)S(1)}, u32[]{:S(2)}, u32[]{:S(2)}) async-start(s32[1,8,128]{2,0,1:T(1,128)} %bitcast.38), calls=%async_computation | async-start | bytes 8192 | tf_op jit(solution)/shard_map/all_to_all | solution.py:67
  27.8 9.2 %all-to-all-start.1 = ((bf16[32,8,128]{2,0,1:T(8,128)(2,1)}), bf16[32,8,128]{2,0,1:T(8,128)(2,1)S(1)}, u32[]{:S(2)}, u32[]{:S(2)}) async-start(bf16[32,8,128]{2,0,1:T(8,128)(2,1)} %select_bitcast_fusion.1), calls=%async_computation.1 | async-start | bytes 131072 | tf_op jit(solution)/shard_map/all_to_all | solution.py:70
  32.0 66.0 %all-gather.2.cloned.1.call-start = ((), (), s32[]{:S(2)}) async-start(), calls=%async_computation.3 | async-start | bytes 1310720 | tf_op jit(solution)/shard_map/all_gather | solution.py:89
  56.6 43.0 %copy-start.6 = (f32[64]{0:T(128)S(1)}, f32[64]{0:T(128)}, u32[]{:S(2)}) copy-start(f32[64]{0:T(128)} %param.22) | copy-start | bytes 772
  57.0 9.8 %collective-permute-start = (bf16[32,4096]{1,0:T(8,128)(2,1)S(1)}, bf16[32,4096]{1,0:T(8,128)(2,1)S(1)}, u32[]{:S(2)}, u32[]{:S(2)}) collective-permute-start(bf16[32,4096]{1,0:T(8,128)(2,1)S(1)} %get-tuple-element.160), channel_id=1, source_target_pairs={{0,1},{1,2},{2,3},{3,0},{4,5},{5,6},{6,7},{7,4},{8,9},{9,10},{10,1... | collective-permute-start | bytes 786440 | tf_op jit(solution)/shard_map/ppermute | solution.py:19
  59.4 60.8 %reduce-scatter.4.cloned.1.call-start = ((), (), s32[]{:S(2)}) async-start(), calls=%async_computation.4 | async-start | bytes 327680
  66.7 15.8 %collective-permute-start.1 = (bf16[32,4096]{1,0:T(8,128)(2,1)S(1)}, bf16[32,4096]{1,0:T(8,128)(2,1)S(1)}, u32[]{:S(2)}, u32[]{:S(2)}) collective-permute-start(bf16[32,4096]{1,0:T(8,128)(2,1)S(1)} %collective-permute-done), channel_id=1, source_target_pairs={{0,1},{1,2},{2,3},{3,0},{4,5},{5,6},{6,7},{7,4},{8,9},{9,10},{10,1... | collective-permute-start | bytes 786440 | tf_op jit(solution)/shard_map/ppermute | solution.py:19
  82.6 15.4 %collective-permute-start.2 = (bf16[32,4096]{1,0:T(8,128)(2,1)S(1)}, bf16[32,4096]{1,0:T(8,128)(2,1)S(1)}, u32[]{:S(2)}, u32[]{:S(2)}) collective-permute-start(bf16[32,4096]{1,0:T(8,128)(2,1)S(1)} %collective-permute-done.1), channel_id=1, source_target_pairs={{0,1},{1,2},{2,3},{3,0},{4,5},{5,6},{6,7},{7,4},{8,9},{9,10},{10,1... | collective-permute-start | bytes 786440 | tf_op jit(solution)/shard_map/ppermute | solution.py:19
  83.8 17.0 %copy-start.3 = (bf16[256,64]{0,1:T(8,128)(2,1)S(1)}, bf16[256,64]{0,1:T(8,128)(2,1)}, u32[]{:S(2)}) copy-start(bf16[256,64]{0,1:T(8,128)(2,1)} %param.23) | copy-start | bytes 98308
  99.6 2.0 %copy-start.2 = (bf16[256,64]{0,1:T(8,128)(2,1)S(1)}, bf16[256,64]{0,1:T(8,128)(2,1)}, u32[]{:S(2)}) copy-start(bf16[256,64]{0,1:T(8,128)(2,1)} %param.24) | copy-start | bytes 98308
  100.6 20.5 %copy-start.5 = (f32[64]{0:T(128)S(1)}, f32[64]{0:T(128)}, u32[]{:S(2)}) copy-start(f32[64]{0:T(128)} %param.25) | copy-start | bytes 772
Sparse Core Ops, SparseCore 0:
  59.5 35.7 all-gather.1
  102.9 17.2 reduce-scatter.3
